TPU v7x, 32 devices: a whole 2x2x4 slice. The times are simulated.
32 devices in a mesh: rep: 2 (over x), exp: 4 (over z), ten: 4 (over y, core).
Axes of the slice: x: 2, y: 2, z: 4, core: 2. Of those that a mesh axis runs over, the one named last changes fastest.
Arguments:
- hidden_in: bfloat16 [768, 3072], P(('rep', 'exp', 'ten')), parts along dimension 0, may hold values from -6 to 6
- queries: bfloat16 [768, 6144], P(('rep', 'exp', 'ten')), parts along dimension 0, may hold values from -100 to 100
- new_kv: bfloat16 [2, 768, 1024], P(None, ('rep', 'exp', 'ten')), parts along dimension 1, may hold values from -5 to 5
- prefix_kv: bfloat16 [2, 8, 128, 1024], P(None, ('rep', 'exp'), 'ten'), parts along dimension 1, may hold values from -5 to 5
- decode_kv: bfloat16 [2, 128, 48, 1024], P(None, ('rep', 'exp', 'ten')), parts along dimension 1, may hold values from -5 to 5
- prefix_len: int32 [8], P(('rep', 'exp')), parts along dimension 0, may hold values from 2 to 128
- decode_len: int32 [128], P(('rep', 'exp', 'ten')), parts along dimension 0, may hold values from 2 to 48
- out_proj: bfloat16 [6144, 3072], P('ten'), may hold values from -0.078125 to 0.078125
- norm_gain: float32 [3072], replicated, may hold values from 0.5 to 1.5
- router_w: bfloat16 [3072, 8], replicated, may hold values from -0.109375 to 0.109375
- expert_ids: int32 [768, 2], P(('rep', 'exp', 'ten')), parts along dimension 0, may hold values from 0 to 7, all different within a row; in each aligned block of 24 rows (0 to 23, 24 to 47, ...) at most 7 rows name the same one
- w_gate: bfloat16 [8, 3072, 8192], P('exp', None, 'ten'), may hold values from -0.109375 to 0.109375
- w_up: bfloat16 [8, 3072, 8192], P('exp', None, 'ten'), may hold values from -0.109375 to 0.109375
- w_down: bfloat16 [8, 8192, 3072], P('exp', 'ten'), may hold values from -0.0625 to 0.0625
Outputs:
- layer_out: bfloat16 [768, 3072], P(('rep', 'exp', 'ten')), parts along dimension 0
There are 2 independent parts, one for each index of `rep`. A program takes and returns all parts, laid end to end along the dimension named above; an argument that names none is the same for every part. Nothing has to cross between parts.
Inputs may be any that keep to these rules, and one draw needn't show every extreme that they name: `expert_ids`: each row names two different experts. Within each aligned block of 24 rows (the rows of one device) no expert is named by more than 7 rows, and in some block one expert is named by exactly 7 rows.
All inputs are finite; a program needn't handle non-finite values.
Results may differ from a plain program's by a relative error of at most 0.013.
Values may be sent and summed in bfloat16 or wider, within the bound.
No kernel may reach another device: no remote copies, remote signals or barrier semaphores. Data moves between devices by JAX's collectives and lax.ppermute only.
A program may use at most 128 MiB of HBM per device.

v0:
```python
import jax
import jax.numpy as jnp
from jax import lax
from jax.sharding import PartitionSpec as P

HD = 128
CAP = 7
lowest_score = -1e30


def local_softmax(scores, visible):
    masked = jnp.where(visible, scores, lowest_score)
    row_max = jnp.max(masked, axis=-1)
    exponent = jnp.where(visible, jnp.exp(masked - row_max[..., None]), 0.0)
    return (row_max, exponent, jnp.sum(exponent, axis=-1))


def on_device(
    hidden_in,
    queries,
    new_kv,
    prefix_kv,
    decode_kv,
    prefix_len,
    decode_len,
    out_proj,
    norm_gain,
    router_w,
    expert_ids,
    w_gate,
    w_up,
    w_down,
):
    ten_size = lax.axis_size("ten")
    groups = lax.axis_size("exp")
    my_ten = lax.axis_index("ten")
    rows_dev, model_width = hidden_in.shape
    dec_dev = decode_len.shape[0]
    span_dev = rows_dev - dec_dev
    span_rows = span_dev * ten_size
    kv_width = new_kv.shape[2]
    heads_kv = kv_width // HD
    heads_q = queries.shape[1] // HD
    per_kv = heads_q // heads_kv
    score_scale = HD ** (-0.5)
    ctx_len = decode_kv.shape[2]
    own_heads = queries.reshape(rows_dev, heads_kv, per_kv, HD)
    dec_keys = jnp.concatenate([decode_kv[0], new_kv[0, span_dev:, None]], axis=1).reshape(
        dec_dev, ctx_len + 1, heads_kv, HD
    )
    dec_values = jnp.concatenate([decode_kv[1], new_kv[1, span_dev:, None]], axis=1).reshape(
        dec_dev, ctx_len + 1, heads_kv, HD
    )
    dec_scores = (
        jnp.einsum(
            "dcgh,dpch->dcgp", own_heads[span_dev:], dec_keys, preferred_element_type=jnp.float32
        )
        * score_scale
    )
    dec_pos = jnp.arange(ctx_len + 1, dtype=jnp.int32)[None, :]
    dec_visible = ((dec_pos < decode_len[:, None]) | (dec_pos == ctx_len))[:, None, None, :]
    dec_max, dec_exponent, dec_totals = local_softmax(dec_scores, dec_visible)
    dec_partial = jnp.einsum(
        "dcgp,dpch->dcgh",
        dec_exponent.astype(jnp.bfloat16),
        dec_values,
        preferred_element_type=jnp.float32,
    )
    full_prefix, full_fresh = (
        lax.all_gather(prefix_kv[:, 0], "ten", axis=1, tiled=True),
        lax.all_gather(new_kv[:, :span_dev], "ten", axis=1, tiled=True),
    )
    prefix_total = full_prefix.shape[1]
    key_rows = jnp.concatenate([full_prefix[0], full_fresh[0]], axis=0).reshape(
        prefix_total + span_rows, heads_kv, HD
    )
    value_rows = jnp.concatenate([full_prefix[1], full_fresh[1]], axis=0).reshape(
        prefix_total + span_rows, heads_kv, HD
    )
    scores = (
        jnp.einsum(
            "rcgh,pch->rcgp", own_heads[:span_dev], key_rows, preferred_element_type=jnp.float32
        )
        * score_scale
    )
    query_row = my_ten * span_dev + jnp.arange(span_dev, dtype=jnp.int32)[:, None]
    positions = jnp.arange(prefix_total + span_rows, dtype=jnp.int32)[None, :]
    visible = jnp.where(
        positions < prefix_total, positions < prefix_len[0], positions - prefix_total <= query_row
    )[:, None, None, :]
    row_max, exponent, totals = local_softmax(scores, visible)
    span_out = (
        jnp.einsum(
            "rcgp,pch->rcgh",
            exponent.astype(jnp.bfloat16),
            value_rows,
            preferred_element_type=jnp.float32,
        )
        / totals[..., None]
    )
    dec_out = dec_partial / dec_totals[..., None]
    attended_rows = (
        jnp.concatenate([span_out, dec_out], axis=0)
        .reshape(rows_dev, heads_q * HD)
        .astype(jnp.bfloat16)
    )
    attended = lax.all_to_all(attended_rows, "ten", split_axis=1, concat_axis=0, tiled=True)
    row_block = attended
    projected = lax.psum_scatter(
        jnp.dot(row_block, out_proj, preferred_element_type=jnp.float32).astype(jnp.bfloat16),
        "ten",
        scatter_dimension=0,
        tiled=True,
    ).astype(jnp.float32)
    residual = hidden_in.astype(jnp.float32) + projected
    mean_square = jnp.mean(residual * residual, axis=1, keepdims=True)
    normed = (residual * lax.rsqrt(mean_square + 1e-05) * norm_gain).astype(jnp.bfloat16)
    logits = jnp.dot(normed, router_w, preferred_element_type=jnp.float32)
    experts = router_w.shape[1]
    chosen_hot = (expert_ids[:, :, None] == jnp.arange(experts, dtype=jnp.int32)).astype(jnp.int32)
    chosen_logits = jnp.sum(jnp.where(chosen_hot == 1, logits[:, None, :], 0.0), axis=2)
    route_weights = jax.nn.softmax(chosen_logits, axis=1)
    flat_hot = chosen_hot.reshape(rows_dev * 2, experts)
    slot_rank = jnp.sum((jnp.cumsum(flat_hot, axis=0) - flat_hot) * flat_hot, axis=1).reshape(
        rows_dev, 2
    )
    capacity = CAP
    slot_index = jnp.arange(capacity, dtype=jnp.int32)
    assignment = chosen_hot[:, :, :, None] * (slot_rank[:, :, None, None] == slot_index).astype(
        jnp.int32
    )
    placement = jnp.sum(assignment, axis=1)
    local_experts = experts // groups
    placement_split = placement.reshape(rows_dev, groups, local_experts, capacity).astype(
        jnp.bfloat16
    )
    outgoing = jnp.einsum(
        "rnlc,rd->lncd", placement_split, normed, preferred_element_type=jnp.float32
    ).astype(jnp.bfloat16)
    arrived = lax.all_to_all(outgoing, "exp", split_axis=1, concat_axis=1, tiled=True)
    shard_rows = lax.all_gather(arrived, "ten", axis=1, tiled=True)
    gate_act = jnp.einsum("lscd,ldf->lscf", shard_rows, w_gate, preferred_element_type=jnp.float32)
    up_act = jnp.einsum("lscd,ldf->lscf", shard_rows, w_up, preferred_element_type=jnp.float32)
    hidden = (jax.nn.silu(gate_act) * up_act).astype(jnp.bfloat16)
    row_block = hidden
    summed = lax.psum_scatter(
        jnp.einsum("lscf,lfd->slcd", row_block, w_down, preferred_element_type=jnp.float32).astype(
            jnp.bfloat16
        ),
        "ten",
        scatter_dimension=0,
        tiled=True,
    )
    returned = lax.all_to_all(summed, "exp", split_axis=0, concat_axis=0, tiled=True)
    outputs = returned.reshape(experts * capacity, model_width).astype(jnp.float32)
    weight_map = jnp.sum(
        assignment.astype(jnp.float32) * route_weights[:, :, None, None], axis=1
    ).reshape(rows_dev, experts * capacity)
    expert_mix = jnp.dot(
        weight_map, outputs, precision=lax.Precision.HIGHEST, preferred_element_type=jnp.float32
    )
    return (residual + expert_mix).astype(jnp.bfloat16)


def solution(mesh):
    in_specs = (
        P(("rep", "exp", "ten"), None),
        P(("rep", "exp", "ten"), None),
        P(None, ("rep", "exp", "ten"), None),
        P(None, ("rep", "exp"), "ten", None),
        P(None, ("rep", "exp", "ten"), None, None),
        P(("rep", "exp")),
        P(("rep", "exp", "ten")),
        P("ten", None),
        P(),
        P(),
        P(("rep", "exp", "ten"), None),
        P("exp", None, "ten"),
        P("exp", None, "ten"),
        P("exp", "ten", None),
    )
    out_specs = P(("rep", "exp", "ten"), None)
    return jax.shard_map(
        on_device, mesh=mesh, in_specs=in_specs, out_specs=out_specs, check_vma=False
    )
```

profile of v0, /device:TPU:0, one launch (start us, length us, event | category | flops | bytes accessed | tf_op | source)
XLA Modules:
  0.0 201.0 jit_solution(10028590843201728159)
XLA Ops:
  6.6 0.8 fusion.119
  7.3 1.2 fusion.117
  10.1 7.6 %all_gather.10 = bf16[2,80,1024]{2,0,1:T(2,128)(2,1)S(1)} all-gather(bf16[2,20,1024]{2,0,1:T(2,128)(2,1)S(1)} %copy.122), channel_id=1, replica_groups=mesh['rep'=2,'exp'=4,'ten'=4] {'ten'}, dimensions={1}, use_global_device_ids=true | all-gather | bytes 409600 | tf_op jit(solution)/shard_map/all_gather | solution.py:71
  17.7 1.4 slice_reduce_fusion
  19.3 7.3 %all-gather = bf16[2,1,128,1024]{3,0,1,2:T(2,128)(2,1)S(1)} all-gather(bf16[2,1,32,1024]{3,0,1,2:T(2,128)(2,1)S(1)} %copy.87), channel_id=2, replica_groups=mesh['rep'=2,'exp'=4,'ten'=4] {'ten'}, dimensions={2}, use_global_device_ids=true | all-gather | bytes 655360 | tf_op jit(solution)/shard_map/all_gather | solution.py:70
  26.6 0.7 fusion.118
  30.4 0.7 fusion.123
  31.2 0.8 fusion.35
  32.3 8.8 %all_to_all.26 = bf16[24,4,1536]{2,0,1:T(8,128)(2,1)S(1)} all-to-all(bf16[24,4,1536]{2,0,1:T(8,128)(2,1)S(1)} %copy.103), channel_id=1, replica_groups=mesh['rep'=2,'exp'=4,'ten'=4] {'ten'}, dimensions={1} | all-to-all | bytes 589824 | tf_op jit(solution)/shard_map/all_to_all | solution.py:107
  41.1 6.2 %convolution_convert_fusion = bf16[96,3072]{1,0:T(8,128)(2,1)} fusion(bf16[96,1536]{1,0:T(8,128)(2,1)S(1)} %bitcast.127, bf16[1536,3072]{1,0:T(8,128)(2,1)} %param.21), kind=kOutput, calls=%fused_computation.10 | convolution fusion | flops 906264576 | bytes 10321920 | tf_op jit(solution)/shard_map/dot_general | solution.py:110
  49.4 20.6 %reduce-scatter.3.cloned.1.call-done = bf16[24,3072]{1,0:T(8,128)(2,1)} async-done(((bf16[96,3072]{1,0:T(8,128)(2,1)}), bf16[24,3072]{1,0:T(8,128)(2,1)}) %reduce-scatter.3.cloned.1.call-update) | async-done | bytes 147472 | tf_op jit(solution)/shard_map/reduce_scatter | solution.py:109
  70.0 1.1 multiply_reduce_fusion
  71.0 1.0 multiply_convert_fusion
  72.7 14.9 %all_to_all.27 = bf16[2,4,7,3072]{3,0,2,1:T(2,128)(2,1)} all-to-all(bf16[2,4,7,3072]{3,0,2,1:T(2,128)(2,1)S(1)} %copy.108), channel_id=1, replica_groups=mesh['rep'=2,'exp'=4,'ten'=4] {'exp'}, dimensions={1} | all-to-all | bytes 688128 | tf_op jit(solution)/shard_map/all_to_all | solution.py:140
  87.9 16.6 %all-gather.3.cloned.1.call-done = bf16[2,16,7,3072]{3,0,2,1:T(2,128)(2,1)} async-done(((bf16[2,4,7,3072]{3,0,2,1:T(2,128)(2,1)}), bf16[2,16,7,3072]{3,0,2,1:T(2,128)(2,1)}) %all-gather.3.cloned.1.call-update) | async-done | bytes 1376272 | tf_op jit(solution)/shard_map/all_gather | solution.py:141
  104.5 10.9 %fusion.6 = f32[2,16,7,2048]{3,1,2,0:T(8,128)S(1)} fusion(bf16[2,3072,2048]{2,1,0:T(8,128)(2,1)} %param.25, bf16[2,16,7,3072]{3,0,2,1:T(2,128)(2,1)} %all-gather.3.cloned.1.call-done), kind=kOutput, calls=%fused_computation.6 | convolution fusion | flops 2818572288 | bytes 28377088 | tf_op jit(solution)/shard_map/lscd,ldf->lscf/dot_general | solution.py:142
  115.4 20.2 %fusion.11 = bf16[16,2,7,3072]{3,0,2,1:T(8,128)(2,1)} fusion(bf16[2,2048,3072]{2,1,0:T(8,128)(2,1)} %param.27, bf16[2,3072,2048]{2,1,0:T(8,128)(2,1)} %param.26, f32[2,16,7,2048]{3,1,2,0:T(8,128)S(1)} %fusion.6, bf16[2,16,7,3072]{3,0,2,1:T(2,128)(2,1)S(1)} %copy-done.1), kind=kOutput, calls=%fused_computation.9 | convolution fusion | flops 5640585216 | bytes 54919168 | tf_op jit(solution)/shard_map/lscf,lfd->slcd/dot_general | solution.py:147
  136.3 0.6 dynamic-slice
  137.7 38.1 %all-reduce.3.cloned.1.call-done = bf16[16,2,7,3072]{3,0,2,1:T(8,128)(2,1)} async-done(((bf16[16,2,7,3072]{3,0,2,1:T(8,128)(2,1)}), bf16[16,2,7,3072]{3,0,2,1:T(8,128)(2,1)}) %all-reduce.3.cloned.1.call-update) | async-done | bytes 1376272
  175.9 1.3 constant_dynamic-slice_fusion
  177.1 1.0 copy.111
  178.1 4.6 %all-to-all-start.2 = ((bf16[4,2,7,3072]{3,1,2,0:T(2,128)(2,1)}), bf16[4,2,7,3072]{3,1,2,0:T(2,128)(2,1)S(1)}, u32[]{:S(2)}, u32[]{:S(2)}) async-start(bf16[4,2,7,3072]{3,1,2,0:T(2,128)(2,1)} %copy.111), calls=%async_computation.3 | async-start | bytes 688128 | tf_op jit(solution)/shard_map/all_to_all | solution.py:154
  182.9 10.4 %all-to-all-done.2 = bf16[4,2,7,3072]{3,1,2,0:T(2,128)(2,1)S(1)} async-done(((bf16[4,2,7,3072]{3,1,2,0:T(2,128)(2,1)}), bf16[4,2,7,3072]{3,1,2,0:T(2,128)(2,1)S(1)}, u32[]{:S(2)}, u32[]{:S(2)}) %all-to-all-start.2) | async-done | bytes 344096 | tf_op jit(solution)/shard_map/all_to_all | solution.py:154
  193.5 1.0 fusion.15
  (92 shorter events, 8.3 us)
Async XLA Ops:
  6.5 131.0 %copy-start = (bf16[3072,8]{0,1:T(8,128)(2,1)S(1)}, bf16[3072,8]{0,1:T(8,128)(2,1)}, u32[]{:S(2)}) copy-start(bf16[3072,8]{0,1:T(8,128)(2,1)} %param.23) | copy-start | bytes 147460
  6.5 63.4 %reduce-scatter.3.cloned.1.call-start = ((), (), s32[]{:S(2)}) async-start(), calls=%async_computation.4 | async-start | bytes 737280 | tf_op jit(solution)/shard_map/reduce_scatter | solution.py:109
  7.3 1.4 copy-start.4
  8.6 0.7 copy-start.14
  8.9 1.2 copy-start.5
  9.4 9.8 %copy-start.6 = (bf16[2,1,32,1024]{3,2,1,0:T(8,128)(2,1)S(1)}, bf16[2,1,32,1024]{3,2,1,0:T(8,128)(2,1)}, u32[]{:S(2)}) copy-start(bf16[2,1,32,1024]{3,2,1,0:T(8,128)(2,1)} %param.17) | copy-start | bytes 393220
  41.1 6.3 %copy-start.12 = (s32[24,2]{0,1:T(2,128)S(1)}, s32[24,2]{0,1:T(2,128)}, u32[]{:S(2)}) copy-start(s32[24,2]{0,1:T(2,128)} %param.24) | copy-start | bytes 580
  41.1 28.8 %copy-start.2 = (bf16[24,3072]{1,0:T(8,128)(2,1)S(1)}, bf16[24,3072]{1,0:T(8,128)(2,1)}, u32[]{:S(2)}) copy-start(bf16[24,3072]{1,0:T(8,128)(2,1)} %param.14) | copy-start | bytes 442372
  41.1 29.9 %copy-start.11 = (f32[3072]{0:T(1024)S(1)}, f32[3072]{0:T(1024)}, u32[]{:S(2)}) copy-start(f32[3072]{0:T(1024)} %param.22) | copy-start | bytes 36868
  47.4 57.1 %all-gather.3.cloned.1.call-start = ((), (), s32[]{:S(2)}) async-start(), calls=%async_computation.5 | async-start | bytes 1720320 | tf_op jit(solution)/shard_map/all_gather | solution.py:141
  48.2 0.6 copy-start.7
  48.8 0.6 copy-start.9
  87.7 88.2 %all-reduce.3.cloned.1.call-start = ((), (), s32[]{:S(2)}) async-start(), calls=%async_computation.6 | async-start | bytes 2752512
  104.5 10.9 %copy-start.1 = (bf16[2,16,7,3072]{3,0,2,1:T(2,128)(2,1)S(1)}, bf16[2,16,7,3072]{3,0,2,1:T(2,128)(2,1)}, u32[]{:S(2)}) copy-start(bf16[2,16,7,3072]{3,0,2,1:T(2,128)(2,1)} %all-gather.3.cloned.1.call-done) | copy-start | bytes 4128772
  135.6 0.7 copy-start.15
  135.7 47.1 %copy-start.13 = (s32[24,2]{0,1:T(2,128)S(1)}, s32[24,2]{0,1:T(2,128)}, u32[]{:S(2)}) copy-start(s32[24,2]{0,1:T(2,128)} %param.24) | copy-start | bytes 580
  135.7 47.1 %copy-start.8 = (s32[24,2,8]{0,2,1:T(8,128)S(1)}, s32[24,2,8]{0,2,1:T(8,128)}, u32[]{:S(2)}) copy-start(s32[24,2,8]{0,2,1:T(8,128)} %copy-done.7) | copy-start | bytes 4612
  135.7 47.1 %copy-start.10 = (s32[24,2,7]{0,2,1:T(8,128)S(1)}, s32[24,2,7]{0,2,1:T(8,128)}, u32[]{:S(2)}) copy-start(s32[24,2,7]{0,2,1:T(8,128)} %copy-done.9) | copy-start | bytes 4036
  177.1 16.3 %copy-start.3 = (bf16[24,3072]{1,0:T(8,128)(2,1)S(1)}, bf16[24,3072]{1,0:T(8,128)(2,1)}, u32[]{:S(2)}) copy-start(bf16[24,3072]{1,0:T(8,128)(2,1)} %reduce-scatter.3.cloned.1.call-done) | copy-start | bytes 442372
  178.1 15.1 %all-to-all-start.2 = ((bf16[4,2,7,3072]{3,1,2,0:T(2,128)(2,1)}), bf16[4,2,7,3072]{3,1,2,0:T(2,128)(2,1)S(1)}, u32[]{:S(2)}, u32[]{:S(2)}) async-start(bf16[4,2,7,3072]{3,1,2,0:T(2,128)(2,1)} %copy.111), calls=%async_computation.3 | async-start | bytes 688128 | tf_op jit(solution)/shard_map/all_to_all | solution.py:154
Sparse Core Ops, SparseCore 0:
  47.5 22.3 reduce-scatter.2
  87.8 16.6 all-gather.2
  135.8 40.0 all-reduce.2
where the time goes:
time: 201 us
  waiting for transfers between devices  85.7 us (43%)
  matrix products  41.3 us (21%)
  blocking collectives  38.6 us (19%)
  between operations  14.8 us (7%)
  local copies, waits for them, and re-layouts  12.7 us (6%)
  starting transfers between devices  4.87 us (2%)
  other arithmetic  2.9 us (1%)
    unnamed x4, waiting for transfers between devices  38.2 us
    reduce_scatter x1, waiting for transfers between devices, on_device(): lax.psum_scatter(jnp.dot(row_block, out_proj, preferred_element_type=jnp....  20.6 us
    dot_general x1, matrix products, on_device(): jnp.einsum('lscf,lfd->slcd', row_block, w_down, preferred_element_type=jn...  20.2 us
    all_gather x1, waiting for transfers between devices, on_device(): shard_rows = lax.all_gather(arrived, 'ten', axis=1, tiled=True)  16.6 us
    all_to_all x1, blocking collectives, on_device(): lax.all_to_all(outgoing, 'exp', split_axis=1, concat_axis=1, tiled=True)  14.9 us
    dot_general x1, matrix products, on_device(): jnp.einsum('lscd,ldf->lscf', shard_rows, w_gate, preferred_element_type=j...  10.9 us
    all_to_all x1, waiting for transfers between devices, on_device(): lax.all_to_all(summed, 'exp', split_axis=0, concat_axis=0, tiled=True)  10.4 us
    all_to_all x1, blocking collectives, on_device(): lax.all_to_all(attended_rows, 'ten', split_axis=1, concat_axis=0, tiled=T...  8.78 us
  transfers between devices with their start and end apart: 4, of which 4 were waited for; matrix products, arithmetic and copies ran while one was open for 1% of the time, Pallas kernels for 0%

commit v1 on v0

--- a/solution.py
+++ b/solution.py
@@ -151,7 +151,19 @@
         scatter_dimension=0,
         tiled=True,
     )
-    returned = lax.all_to_all(summed, "exp", split_axis=0, concat_axis=0, tiled=True)
+    ways, here = (lax.axis_size("exp"), lax.axis_index("exp"))
+    width = summed.shape[0] // ways
+    dims = list(summed.shape)
+    dims[0] = width
+    height = dims[0]
+    dims[0] = height * ways
+    full = jnp.zeros(dims, summed.dtype)
+    for mask in range(ways):
+        part = lax.dynamic_slice_in_dim(summed, (here ^ mask) * width, width, axis=0)
+        if mask:
+            part = lax.ppermute(part, "exp", [(d, d ^ mask) for d in range(ways)])
+        full = lax.dynamic_update_slice_in_dim(full, part, (here ^ mask) * height, axis=0)
+    returned = full
     outputs = returned.reshape(experts * capacity, model_width).astype(jnp.float32)
     weight_map = jnp.sum(
         assignment.astype(jnp.float32) * route_weights[:, :, None, None], axis=1

time: 201 us -> 204 us (1.015)
    ppermute x0 -> x3, waiting for transfers between devices: none -> 12.5 us  [on_device(): part = lax.ppermute(part, 'exp', [(d, d ^ mask) for d in range(ways)])]
    all_to_all x1 -> x0, waiting for transfers between devices: 10.4 us -> none  [on_device(): lax.all_to_all(summed, 'exp', split_axis=0, concat_axis=0, tiled=True)]
    all_to_all x1 -> x0, starting transfers between devices: 4.6 us -> none  [on_device(): lax.all_to_all(summed, 'exp', split_axis=0, concat_axis=0, tiled=True)]
    ppermute x0 -> x3, starting transfers between devices: none -> 4.45 us  [on_device(): part = lax.ppermute(part, 'exp', [(d, d ^ mask) for d in range(ways)])]
    dynamic_slice x0 -> x1, local copies, waits for them, and re-layouts: none -> 2.65 us  [on_device(): lax.dynamic_slice_in_dim(summed, (here ^ mask) * width, width, axis=0)]
    unnamed x41 -> x40, local copies, waits for them, and re-layouts: 5.37 us -> 4.93 us
  transfers between devices with their start and end apart: 4 -> 6, of which waited for: 4 -> 5; matrix products, arithmetic and copies ran while one was open for 1% -> 1% of each run, Pallas kernels for 0% -> 0%
where the time goes in v1:
time: 204 us; the launch traced here: 203 us
  waiting for transfers between devices  87.7 us (43%)
  matrix products  41.3 us (20%)
  blocking collectives  38.6 us (19%)
  between operations  14.9 us (7%)
  local copies, waits for them, and re-layouts  13 us (6%)
  starting transfers between devices  4.72 us (2%)
  other arithmetic  2.91 us (1%)
    unnamed x4, waiting for transfers between devices  39.4 us
    reduce_scatter x1, waiting for transfers between devices, on_device(): lax.psum_scatter(jnp.dot(row_block, out_proj, preferred_element_type=jnp....  20.6 us
    dot_general x1, matrix products, on_device(): jnp.einsum('lscf,lfd->slcd', row_block, w_down, preferred_element_type=jn...  20.2 us
    all_gather x1, waiting for transfers between devices, on_device(): shard_rows = lax.all_gather(arrived, 'ten', axis=1, tiled=True)  15.2 us
    all_to_all x1, blocking collectives, on_device(): lax.all_to_all(outgoing, 'exp', split_axis=1, concat_axis=1, tiled=True)  15 us
    ppermute x3, waiting for transfers between devices, on_device(): part = lax.ppermute(part, 'exp', [(d, d ^ mask) for d in range(ways)])  12.5 us
    dot_general x1, matrix products, on_device(): jnp.einsum('lscd,ldf->lscf', shard_rows, w_gate, preferred_element_type=j...  10.9 us
    all_to_all x1, blocking collectives, on_device(): lax.all_to_all(attended_rows, 'ten', split_axis=1, concat_axis=0, tiled=T...  8.77 us
  transfers between devices with their start and end apart: 6, of which 5 were waited for; matrix products, arithmetic and copies ran while one was open for 1% of the time, Pallas kernels for 0%

profile of v1, /device:TPU:0, one launch (start us, length us, event | category | flops | bytes accessed | tf_op | source)
XLA Modules:
  0.0 203.2 jit_solution(1401745576272824365)
XLA Ops:
  6.6 0.8 fusion.119
  7.4 1.0 copy.105
  8.3 7.6 %all_gather.10 = bf16[2,80,1024]{2,0,1:T(2,128)(2,1)S(1)} all-gather(bf16[2,20,1024]{2,0,1:T(2,128)(2,1)S(1)} %copy.105), channel_id=1, replica_groups=mesh['rep'=2,'exp'=4,'ten'=4] {'ten'}, dimensions={1}, use_global_device_ids=true | all-gather | bytes 409600 | tf_op jit(solution)/shard_map/all_gather | solution.py:71
  15.9 1.4 slice_reduce_fusion
  18.2 7.3 %all-gather = bf16[2,1,128,1024]{3,0,1,2:T(2,128)(2,1)S(1)} all-gather(bf16[2,1,32,1024]{3,0,1,2:T(2,128)(2,1)S(1)} %copy.68), channel_id=2, replica_groups=mesh['rep'=2,'exp'=4,'ten'=4] {'ten'}, dimensions={2}, use_global_device_ids=true | all-gather | bytes 655360 | tf_op jit(solution)/shard_map/all_gather | solution.py:70
  25.5 0.7 fusion.118
  30.2 0.7 fusion.123
  31.0 0.8 fusion.35
  32.2 8.8 %all_to_all.21 = bf16[24,4,1536]{2,0,1:T(8,128)(2,1)S(1)} all-to-all(bf16[24,4,1536]{2,0,1:T(8,128)(2,1)S(1)} %copy.84), channel_id=1, replica_groups=mesh['rep'=2,'exp'=4,'ten'=4] {'ten'}, dimensions={1} | all-to-all | bytes 589824 | tf_op jit(solution)/shard_map/all_to_all | solution.py:107
  40.9 6.3 %convolution_convert_fusion = bf16[96,3072]{1,0:T(8,128)(2,1)} fusion(bf16[96,1536]{1,0:T(8,128)(2,1)S(1)} %bitcast.127, bf16[1536,3072]{1,0:T(8,128)(2,1)} %param.21), kind=kOutput, calls=%fused_computation.10 | convolution fusion | flops 906264576 | bytes 10321920 | tf_op jit(solution)/shard_map/dot_general | solution.py:110
  49.2 20.6 %reduce-scatter.3.cloned.1.call-done = bf16[24,3072]{1,0:T(8,128)(2,1)} async-done(((bf16[96,3072]{1,0:T(8,128)(2,1)}), bf16[24,3072]{1,0:T(8,128)(2,1)}) %reduce-scatter.3.cloned.1.call-update) | async-done | bytes 147472 | tf_op jit(solution)/shard_map/reduce_scatter | solution.py:109
  69.8 1.1 multiply_reduce_fusion
  70.9 1.0 multiply_convert_fusion
  72.5 15.0 %all_to_all.22 = bf16[2,4,7,3072]{3,0,2,1:T(2,128)(2,1)} all-to-all(bf16[2,4,7,3072]{3,0,2,1:T(2,128)(2,1)S(1)} %copy.89), channel_id=1, replica_groups=mesh['rep'=2,'exp'=4,'ten'=4] {'exp'}, dimensions={1} | all-to-all | bytes 688128 | tf_op jit(solution)/shard_map/all_to_all | solution.py:140
  89.1 15.2 %all-gather.3.cloned.1.call-done = bf16[2,16,7,3072]{3,0,2,1:T(2,128)(2,1)} async-done(((bf16[2,4,7,3072]{3,0,2,1:T(2,128)(2,1)}), bf16[2,16,7,3072]{3,0,2,1:T(2,128)(2,1)}) %all-gather.3.cloned.1.call-update) | async-done | bytes 1376272 | tf_op jit(solution)/shard_map/all_gather | solution.py:141
  104.3 10.9 %fusion.6 = f32[2,16,7,2048]{3,1,2,0:T(8,128)S(1)} fusion(bf16[2,3072,2048]{2,1,0:T(8,128)(2,1)} %param.25, bf16[2,16,7,3072]{3,0,2,1:T(2,128)(2,1)} %all-gather.3.cloned.1.call-done), kind=kOutput, calls=%fused_computation.6 | convolution fusion | flops 2818572288 | bytes 28377088 | tf_op jit(solution)/shard_map/lscd,ldf->lscf/dot_general | solution.py:142
  115.3 20.2 %fusion.11 = bf16[16,2,7,3072]{3,0,2,1:T(8,128)(2,1)} fusion(bf16[2,2048,3072]{2,1,0:T(8,128)(2,1)} %param.27, bf16[2,3072,2048]{2,1,0:T(8,128)(2,1)} %param.26, f32[2,16,7,2048]{3,1,2,0:T(8,128)S(1)} %fusion.6, bf16[2,16,7,3072]{3,0,2,1:T(2,128)(2,1)S(1)} %copy-done.1), kind=kOutput, calls=%fused_computation.9 | convolution fusion | flops 5640585216 | bytes 54919168 | tf_op jit(solution)/shard_map/lscf,lfd->slcd/dot_general | solution.py:147
  136.3 39.4 %all-reduce.3.cloned.1.call-done = bf16[16,2,7,3072]{3,0,2,1:T(8,128)(2,1)} async-done(((bf16[16,2,7,3072]{3,0,2,1:T(8,128)(2,1)}), bf16[16,2,7,3072]{3,0,2,1:T(8,128)(2,1)}) %all-reduce.3.cloned.1.call-update) | async-done | bytes 1376272
  175.7 2.6 %constant_dynamic-slice_fusion.3 = (bf16[1,2,7,3072]{3,0,2,1:T(2,128)(2,1)S(1)}, bf16[1,2,7,3072]{3,0,2,1:T(2,128)(2,1)S(1)}, bf16[1,2,7,3072]{3,0,2,1:T(2,128)(2,1)S(1)}, bf16[1,2,7,3072]{3,0,2,1:T(2,128)(2,1)S(1)}) fusion(bf16[16,2,7,3072]{3,0,2,1:T(8,128)(2,1)} %all-reduce.3.cloned.1.call-done, s32[]{:T(128)S(6)} %add.79, s32[]{:T(128)S(6)} %add.75, ...), kind=kLoop, calls=%fused_computation.88 | loop fusion | bytes 688144 | tf_op jit(solution)/shard_map/dynamic_slice | solution.py:162
  178.4 1.6 collective-permute-start
  179.9 2.4 %collective-permute-start.1 = (bf16[1,2,7,3072]{3,0,2,1:T(2,128)(2,1)S(1)}, bf16[1,2,7,3072]{3,0,2,1:T(2,128)(2,1)S(1)}, u32[]{:S(2)}, u32[]{:S(2)}) collective-permute-start(bf16[1,2,7,3072]{3,0,2,1:T(2,128)(2,1)S(1)} %get-tuple-element.8), channel_id=1, source_target_pairs={{0,8},{4,12},{8,0},{12,4},{1,9},{5,13},{9,1},{13,5},{2,10},{6,14},... | collective-permute-start | bytes 258056 | tf_op jit(solution)/shard_map/ppermute | solution.py:164
  182.9 4.2 %collective-permute-done = bf16[1,2,7,3072]{3,0,2,1:T(2,128)(2,1)S(1)} collective-permute-done((bf16[1,2,7,3072]{3,0,2,1:T(2,128)(2,1)S(1)}, bf16[1,2,7,3072]{3,0,2,1:T(2,128)(2,1)S(1)}, u32[]{:S(2)}, u32[]{:S(2)}) %collective-permute-start) | collective-permute-done | bytes 86048 | tf_op jit(solution)/shard_map/ppermute | solution.py:164
  187.1 8.3 %collective-permute-done.1 = bf16[1,2,7,3072]{3,0,2,1:T(2,128)(2,1)S(1)} collective-permute-done((bf16[1,2,7,3072]{3,0,2,1:T(2,128)(2,1)S(1)}, bf16[1,2,7,3072]{3,0,2,1:T(2,128)(2,1)S(1)}, u32[]{:S(2)}, u32[]{:S(2)}) %collective-permute-start.1) | collective-permute-done | bytes 86048 | tf_op jit(solution)/shard_map/ppermute | solution.py:164
  195.7 1.0 fusion.15
  (99 shorter events, 9.5 us)
Async XLA Ops:
  6.5 129.0 %copy-start = (bf16[3072,8]{0,1:T(8,128)(2,1)S(1)}, bf16[3072,8]{0,1:T(8,128)(2,1)}, u32[]{:S(2)}) copy-start(bf16[3072,8]{0,1:T(8,128)(2,1)} %param.23) | copy-start | bytes 147460
  6.5 11.5 %copy-start.6 = (bf16[2,1,32,1024]{3,2,1,0:T(8,128)(2,1)S(1)}, bf16[2,1,32,1024]{3,2,1,0:T(8,128)(2,1)}, u32[]{:S(2)}) copy-start(bf16[2,1,32,1024]{3,2,1,0:T(8,128)(2,1)} %param.17) | copy-start | bytes 393220
  6.5 63.2 %reduce-scatter.3.cloned.1.call-start = ((), (), s32[]{:S(2)}) async-start(), calls=%async_computation.3 | async-start | bytes 737280 | tf_op jit(solution)/shard_map/reduce_scatter | solution.py:109
  25.5 1.4 copy-start.5
  26.6 1.2 copy-start.4
  28.0 0.7 copy-start.14
  40.9 6.3 %copy-start.12 = (s32[24,2]{0,1:T(2,128)S(1)}, s32[24,2]{0,1:T(2,128)}, u32[]{:S(2)}) copy-start(s32[24,2]{0,1:T(2,128)} %param.24) | copy-start | bytes 580
  40.9 28.8 %copy-start.2 = (bf16[24,3072]{1,0:T(8,128)(2,1)S(1)}, bf16[24,3072]{1,0:T(8,128)(2,1)}, u32[]{:S(2)}) copy-start(bf16[24,3072]{1,0:T(8,128)(2,1)} %param.14) | copy-start | bytes 442372
  40.9 29.9 %copy-start.11 = (f32[3072]{0:T(1024)S(1)}, f32[3072]{0:T(1024)}, u32[]{:S(2)}) copy-start(f32[3072]{0:T(1024)} %param.22) | copy-start | bytes 36868
  47.2 57.1 %all-gather.3.cloned.1.call-start = ((), (), s32[]{:S(2)}) async-start(), calls=%async_computation.4 | async-start | bytes 1720320 | tf_op jit(solution)/shard_map/all_gather | solution.py:141
  48.0 0.6 copy-start.7
  48.6 0.6 copy-start.9
  70.8 16.9 %copy-start.15 = (u32[32]{0:T(128)S(1)}, u32[32]{0:T(128)}, u32[]{:S(2)}) copy-start(u32[32]{0:T(128)} %constant.63) | copy-start | bytes 388
  87.5 88.2 %all-reduce.3.cloned.1.call-start = ((), (), s32[]{:S(2)}) async-start(), calls=%async_computation.5 | async-start | bytes 2752512
  104.3 10.9 %copy-start.1 = (bf16[2,16,7,3072]{3,0,2,1:T(2,128)(2,1)S(1)}, bf16[2,16,7,3072]{3,0,2,1:T(2,128)(2,1)}, u32[]{:S(2)}) copy-start(bf16[2,16,7,3072]{3,0,2,1:T(2,128)(2,1)} %all-gather.3.cloned.1.call-done) | copy-start | bytes 4128772
  135.5 0.7 copy-start.13
  135.5 0.8 copy-start.8
  135.5 0.8 copy-start.10
  178.3 17.3 %copy-start.3 = (bf16[24,3072]{1,0:T(8,128)(2,1)S(1)}, bf16[24,3072]{1,0:T(8,128)(2,1)}, u32[]{:S(2)}) copy-start(bf16[24,3072]{1,0:T(8,128)(2,1)} %reduce-scatter.3.cloned.1.call-done) | copy-start | bytes 442372
  178.4 8.7 %collective-permute-start = (bf16[1,2,7,3072]{3,0,2,1:T(2,128)(2,1)S(1)}, bf16[1,2,7,3072]{3,0,2,1:T(2,128)(2,1)S(1)}, u32[]{:S(2)}, u32[]{:S(2)}) collective-permute-start(bf16[1,2,7,3072]{3,0,2,1:T(2,128)(2,1)S(1)} %get-tuple-element.9), channel_id=1, source_target_pairs={{0,4},{4,0},{8,12},{12,8},{1,5},{5,1},{9,13},{13,9},{2,6},{6,2},{1... | collective-permute-start | bytes 258056 | tf_op jit(solution)/shard_map/ppermute | solution.py:164
  179.9 15.5 %collective-permute-start.1 = (bf16[1,2,7,3072]{3,0,2,1:T(2,128)(2,1)S(1)}, bf16[1,2,7,3072]{3,0,2,1:T(2,128)(2,1)S(1)}, u32[]{:S(2)}, u32[]{:S(2)}) collective-permute-start(bf16[1,2,7,3072]{3,0,2,1:T(2,128)(2,1)S(1)} %get-tuple-element.8), channel_id=1, source_target_pairs={{0,8},{4,12},{8,0},{12,4},{1,9},{5,13},{9,1},{13,5},{2,10},{6,14},... | collective-permute-start | bytes 258056 | tf_op jit(solution)/shard_map/ppermute | solution.py:164
  182.3 13.2 %collective-permute-start.2 = (bf16[1,2,7,3072]{3,0,2,1:T(2,128)(2,1)S(1)}, bf16[1,2,7,3072]{3,0,2,1:T(2,128)(2,1)S(1)}, u32[]{:S(2)}, u32[]{:S(2)}) collective-permute-start(bf16[1,2,7,3072]{3,0,2,1:T(2,128)(2,1)S(1)} %get-tuple-element.7), channel_id=1, source_target_pairs={{0,12},{4,8},{8,4},{12,0},{1,13},{5,9},{9,5},{13,1},{2,14},{6,10},... | collective-permute-start | bytes 258056 | tf_op jit(solution)/shard_map/ppermute | solution.py:164
Sparse Core Ops, SparseCore 0:
  47.3 22.3 reduce-scatter.2
  87.6 16.6 all-gather.2
  135.6 40.0 all-reduce.2
